TPU v7x, 32 devices: a whole 2x2x4 slice. The times are simulated.
32 devices in a mesh: row: 8 (over y, x, core), col: 4 (over z).
Axes of the slice: x: 2, y: 2, z: 4, core: 2. Of those that a mesh axis runs over, the one named last changes fastest.
Arguments:
- features: bfloat16 [65536, 256], P(('col', 'row')), may hold values from -6 to 6
- block_values: bfloat16 [8, 4, 192, 128, 128], P('row', 'col'), may hold values from -0.1875 to 0.1875
- row_ptr: int32 [8, 4, 65], P('row', 'col'), may hold values from 0 to 144, as said below
- block_cols: int32 [8, 4, 192], P('row', 'col'), may hold values from 0 to 511, as said below
Outputs:
- product: bfloat16 [65536, 256], P(('row', 'col'))
Inputs may be any that keep to these rules, and one draw needn't show every extreme that they name: row_ptr[r, c, 0] = 0, row_ptr never falls along its last dimension, row_ptr[r, c, 64] <= 144, and on exactly one device row_ptr[r, c, 64] = 144. block_cols[r, c, s] lies in c * 128 to (c + 1) * 128 - 1; a block column may repeat within a block row, and repeated blocks add.
All inputs are finite; a program needn't handle non-finite values.
Results may differ from a plain program's by a relative error of at most 0.001.
Values may be sent and summed in bfloat16 or wider, within the bound.
A program may use at most 128 MiB of HBM per device.

v0:
```python
import jax
import jax.numpy as jnp
from jax import lax
from jax.sharding import PartitionSpec as P


def row_weights(pointers, slot_count):
    slot_ids = jnp.arange(slot_count, dtype=jnp.int32)
    inside = (pointers[:-1, None] <= slot_ids[None, :]) & (slot_ids[None, :] < pointers[1:, None])
    return inside.astype(jnp.float32)


def local(features, block_values, row_ptr, block_cols):
    values = block_values[0, 0]
    pointers = row_ptr[0, 0]
    slot_count = values.shape[0]
    block_size = values.shape[1]
    local_rows = pointers.shape[0] - 1
    group_blocks = features.shape[0] * lax.axis_size("row") // block_size
    columns = block_cols[0, 0] - lax.axis_index("col") * group_blocks
    weights = row_weights(pointers, slot_count)
    panel = lax.all_gather(features, "row", axis=0, tiled=True)
    panel_blocks = panel.reshape(group_blocks, block_size, panel.shape[1])
    blocks = panel_blocks[columns]
    panel_width = blocks.shape[2]
    products = jnp.einsum("sij,sjk->sik", values, blocks, preferred_element_type=jnp.float32)
    summed = jnp.einsum("rs,sik->rik", weights, products, precision=lax.Precision.HIGHEST)
    partial_value = summed.reshape(local_rows * block_size, panel_width)
    return lax.psum_scatter(partial_value, "col", scatter_dimension=0, tiled=True).astype(
        jnp.bfloat16
    )


def solution(mesh):
    return jax.shard_map(
        local,
        mesh=mesh,
        in_specs=(
            P(("col", "row"), None),
            P("row", "col", None, None, None),
            P("row", "col", None),
            P("row", "col", None),
        ),
        out_specs=P(("row", "col"), None),
        check_vma=False,
    )
```

profile of v0, /device:TPU:0, one launch (start us, length us, event | category | flops | bytes accessed | tf_op | source)
XLA Modules:
  0.0 294.7 jit_solution(13050265332513122472)
XLA Ops:
  6.5 0.0 all-gather.2.cloned.1.call-start
  6.5 0.7 all-gather.2.cloned.1.call-update
  7.3 0.0 reduce-scatter.2.cloned.1.call-start
  7.3 0.7 compare_select_fusion
  8.0 0.8 slice_bitcast_fusion.1
  8.8 57.4 %all-gather.2.cloned.1.call-done = bf16[16384,256]{1,0:T(8,128)(2,1)} async-done(((bf16[2048,256]{1,0:T(8,128)(2,1)}), bf16[16384,256]{1,0:T(8,128)(2,1)}) %all-gather.2.cloned.1.call-update) | async-done | bytes 8388624 | tf_op jit(solution)/shard_map/all_gather | solution.py:22
  66.2 11.7 %gather_fusion = bf16[192,128,256]{2,1,0:T(8,128)(2,1)} fusion(bf16[128,128,256]{2,1,0:T(8,128)(2,1)} %bitcast.20, s32[1024]{0:T(1024)S(1)} %pad_clamp_fusion), kind=kCustom, calls=%fused_computation | custom fusion | bytes 25166592 | tf_op jit(solution)/shard_map/gather | solution.py:24
  77.9 13.8 %fusion.2 = f32[192,256,128]{2,1,0:T(8,128)} fusion(bf16[192,128,256]{2,1,0:T(8,128)(2,1)} %gather_fusion, bf16[1,1,192,128,128]{4,3,2,1,0:T(8,128)(2,1)} %param.5), kind=kOutput, calls=%fused_computation.3 | convolution fusion | flops 1610612736 | bytes 44040192 | tf_op jit(solution)/shard_map/sij,sjk->sik/dot_general | solution.py:26
  91.7 24.9 %copy.6 = f32[192,256,128]{1,0,2:T(8,128)} copy(f32[192,256,128]{2,1,0:T(8,128)} %fusion.2) | data formatting | bytes 50331648 | tf_op jit(solution)/shard_map/sij,sjk->sik/dot_general | solution.py:26
  116.6 15.7 %fusion = f32[64,128,256]{2,0,1:T(8,128)S(1)} fusion(f32[192,256,128]{1,0,2:T(8,128)} %copy.6, s32[64]{0:T(128)S(1)} %get-tuple-element.6, s32[64]{0:T(128)S(1)} %get-tuple-element.5), kind=kOutput, calls=%fused_computation.1 | convolution fusion | flops 4831875072 | bytes 33554944 | tf_op jit(solution)/shard_map/rs,sik->rik/dot_general | solution.py:27
  132.3 8.1 %copy.5 = f32[64,128,256]{2,1,0:T(8,128)} copy(f32[64,128,256]{2,0,1:T(8,128)S(1)} %fusion) | data formatting | bytes 16777216 | tf_op jit(solution)/shard_map/rs,sik->rik/dot_general | solution.py:27
  140.3 0.0 reduce-scatter.2.cloned.1.call-update
  140.4 144.8 %reduce-scatter.2.cloned.1.call-done = f32[2048,256]{1,0:T(8,128)} async-done(((f32[8192,256]{1,0:T(8,128)}), f32[2048,256]{1,0:T(8,128)}) %reduce-scatter.2.cloned.1.call-update) | async-done | bytes 2097168 | tf_op jit(solution)/shard_map/reduce_scatter | solution.py:29
  285.2 2.7 convert_element_type.4
  (1 shorter events, 0.0 us)
Async XLA Ops:
  6.5 59.7 %all-gather.2.cloned.1.call-start = ((), (), s32[]{:S(2)}) async-start(), calls=%async_computation.1 | async-start | bytes 9437184 | tf_op jit(solution)/shard_map/all_gather | solution.py:22
  7.3 277.9 %reduce-scatter.2.cloned.1.call-start = ((), (), s32[]{:S(2)}) async-start(), calls=%async_computation.2 | async-start | bytes 10485760 | tf_op jit(solution)/shard_map/reduce_scatter | solution.py:29
Sparse Core Ops, SparseCore 0:
  9.2 56.9 all-gather.1
  140.5 144.6 reduce-scatter.1
where the time goes:
time: 295 us
  waiting for transfers between devices  203 us (69%)
  local copies, waits for them, and re-layouts  45.4 us (15%)
  matrix products  29.5 us (10%)
  between operations  13.4 us (5%)
  other arithmetic  3.35 us (1%)
    reduce_scatter x1, waiting for transfers between devices, local(): lax.psum_scatter(partial_value, 'col', scatter_dimension=0, tiled=True)  145 us
    all_gather x1, waiting for transfers between devices, local(): panel = lax.all_gather(features, 'row', axis=0, tiled=True)  57.4 us
    dot_general x1, local copies, waits for them, and re-layouts, local(): jnp.einsum('sij,sjk->sik', values, blocks, preferred_element_type=jnp.flo...  24.9 us
    dot_general x1, matrix products, local(): jnp.einsum('rs,sik->rik', weights, products, precision=lax.Precision.HIGH...  15.7 us
    dot_general x1, matrix products, local(): jnp.einsum('sij,sjk->sik', values, blocks, preferred_element_type=jnp.flo...  13.8 us
    gather x1, local copies, waits for them, and re-layouts, local(): blocks = panel_blocks[columns]  11.7 us
    dot_general x1, local copies, waits for them, and re-layouts, local(): jnp.einsum('rs,sik->rik', weights, products, precision=lax.Precision.HIGH...  8.07 us
  transfers between devices with their start and end apart: 2, of which 2 were waited for; matrix products, arithmetic and copies ran while one was open for 1% of the time, Pallas kernels for 0%

commit v1 on v0

v1 whole, which is shorter than its diff:
```python
import functools

import jax
import jax.numpy as jnp
from jax import lax
from jax.experimental import pallas as pl
from jax.experimental.pallas import tpu as pltpu
from jax.sharding import PartitionSpec as P

LANES = 128
TOP = 32767.0
RIGHT, LEFT = 0, 1


def kernel(
    n_row, n_col, cols, keep, last, filled, features, values_hbm, out,
    panels, values, sums, send_q, recv_q, send_s, recv_s,
    local_sem, ag_send, ag_recv, pair_send, pair_recv, rs_send, rs_recv, sc_send, sc_recv,
):
    n_chips = n_row // 2
    own_blocks = features.shape[0]
    chunks = len(panels)
    live = values.shape[0]
    shard = out.shape[0]
    r, c = lax.axis_index("row"), lax.axis_index("col")
    chip, core = r // 2, r % 2
    partner = chip * 2 + 1 - core

    def slot(k, row):
        return panels[k].at[pl.ds(row * own_blocks, own_blocks)]

    own = [
        pltpu.make_async_copy(
            features.at[:, :, pl.ds(k * LANES, LANES)], slot(k, r), local_sem.at[k]
        )
        for k in range(chunks)
    ]
    for copy in own:
        copy.start()
    fetch = pltpu.make_async_copy(
        values_hbm.at[0, 0, pl.ds(0, live)], values, local_sem.at[chunks]
    )
    fetch.start()

    barrier = pltpu.get_barrier_semaphore()

    def greet(**where):
        pl.semaphore_signal(
            barrier, inc=1, device_id=where, device_id_type=pl.DeviceIdType.MESH
        )

    for o in range(1, n_chips):
        greet(row=((chip + o) % n_chips) * 2 + core)
    greet(row=partner)
    pl.when(c > 0)(lambda: greet(col=c - 1))
    pl.when(c < n_col - 1)(lambda: greet(col=c + 1))
    ends = jnp.where(c > 0, 1, 0) + jnp.where(c < n_col - 1, 1, 0)
    pl.semaphore_wait(barrier, n_chips + ends)

    def remote(src, dst, send, recv, **where):
        return pltpu.make_async_remote_copy(
            src_ref=src, dst_ref=dst, send_sem=send, recv_sem=recv,
            device_id=where, device_id_type=pl.DeviceIdType.MESH,
        )

    def across(k, o):
        target = ((chip + o) % n_chips) * 2 + core
        return remote(slot(k, r), slot(k, r), ag_send.at[k, o], ag_recv.at[k, o], row=target)

    def arriving(k, o):
        row = ((chip + n_chips - o) % n_chips) * 2 + core
        return remote(slot(k, row), slot(k, row), ag_send.at[k, o], ag_recv.at[k, o], row=row)

    def pair(k, o):
        row = ((chip + n_chips - o) % n_chips) * 2 + core
        return remote(slot(k, row), slot(k, row), pair_send.at[k, o], pair_recv.at[k, o], row=partner)

    def pair_arriving(k, o):
        row = ((chip + n_chips - o) % n_chips) * 2 + 1 - core
        return remote(slot(k, row), slot(k, row), pair_send.at[k, o], pair_recv.at[k, o], row=partner)

    def gather_start(k):
        own[k].wait()
        for o in range(1, n_chips):
            across(k, o).start()
        pair(k, 0).start()

    def gather_finish(k):
        for o in range(1, n_chips):
            arriving(k, o).wait_recv()
            pair(k, o).start()
        for o in range(n_chips):
            pair_arriving(k, o).wait_recv()

    unroll = 4 if live % 4 == 0 else 1

    def compute(k):
        def step(i, total):
            first = i * unroll
            products = [
                jnp.dot(
                    values[first + u], panels[k][cols[first + u]],
                    preferred_element_type=jnp.float32,
                )
                for u in range(unroll)
            ]
            for u in range(unroll):
                total = total * keep[first + u] + products[u]
                sums[k, first + u] = total
            return total

        lax.fori_loop(0, live // unroll, step, jnp.zeros(sums.shape[2:], jnp.float32))

    def row_sum(k, q):
        return sums[k, last[q]] * filled[q]

    def received(way, k, j, b):
        levels = recv_q[way, k, j, b].astype(jnp.int32).astype(jnp.float32)
        return levels * recv_s[way, k, j, pl.ds(b, 1), :]

    def message(way, k, j):
        to = c + 1 if way == RIGHT else c - 1
        return (
            remote(send_q.at[way, k, j], recv_q.at[way, k, j],
                   rs_send.at[way, k, j], rs_recv.at[way, k, j], col=to),
            remote(send_s.at[way, k, j], recv_s.at[way, k, j],
                   sc_send.at[way, k, j], sc_recv.at[way, k, j], col=to),
        )

    def forward(way, k, j, incoming):
        if incoming:
            for copy in message(way, k, j):
                copy.wait_recv()

        def one(b, carry):
            x = row_sum(k, j * shard + b)
            if incoming:
                x = x + received(way, k, j, b)
            most = jnp.maximum(jnp.max(jnp.abs(x), axis=0, keepdims=True), 1e-30)
            send_s[way, k, j, pl.ds(b, 1), :] = most * (1.0 / TOP)
            send_q[way, k, j, b] = jnp.round(x * (TOP / most)).astype(jnp.int32).astype(jnp.int16)
            return carry

        lax.fori_loop(0, shard, one, 0)
        for copy in message(way, k, j):
            copy.start()

    def scatter_ends(k):
        @pl.when(c == 0)
        def _():
            for j in range(n_col - 1, 0, -1):
                forward(RIGHT, k, j, False)

        @pl.when(c == n_col - 1)
        def _():
            for j in range(n_col - 1):
                forward(LEFT, k, j, False)

    def scatter_step(k, u):
        right = n_col - 1 - u + c
        left = u - (n_col - 1 - c)

        @pl.when((c > 0) & (right <= n_col - 1) & (right > c))
        def _():
            forward(RIGHT, k, right, True)

        @pl.when((c < n_col - 1) & (left >= 0) & (left < c))
        def _():
            forward(LEFT, k, left, True)

    def finish(k):
        def write(ways):
            for way in ways:
                for copy in message(way, k, c):
                    copy.wait_recv()

            def one(b, carry):
                x = row_sum(k, c * shard + b)
                for way in ways:
                    x = x + received(way, k, c, b)
                out[b, :, pl.ds(k * LANES, LANES)] = x.astype(out.dtype)
                return carry

            lax.fori_loop(0, shard, one, 0)

        pl.when(c == 0)(lambda: write((LEFT,)))
        pl.when(c == n_col - 1)(lambda: write((RIGHT,)))
        pl.when((c > 0) & (c < n_col - 1))(lambda: write((RIGHT, LEFT)))

    gather_start(0)
    fetch.wait()
    gather_finish(0)
    for k in range(chunks):
        if k + 1 < chunks:
            gather_start(k + 1)
        compute(k)
        scatter_ends(k)
        if k > 0:
            for u in range(2, n_col - 1):
                scatter_step(k - 1, u)
            finish(k - 1)
        scatter_step(k, 1)
        if k + 1 < chunks:
            gather_finish(k + 1)
    for u in range(2, n_col - 1):
        scatter_step(chunks - 1, u)
    finish(chunks - 1)

    for k in range(chunks):
        for o in range(n_chips):
            if o > 0:
                across(k, o).wait_send()
            pair(k, o).wait_send()
        for j in range(n_col):
            for way, sent in ((RIGHT, c < j), (LEFT, c > j)):
                @pl.when(sent)
                def _(way=way, k=k, j=j):
                    for copy in message(way, k, j):
                        copy.wait_send()


def local(n_row, n_col, features, block_values, row_ptr, block_cols):
    pointers = row_ptr[0, 0]
    slots, block = block_values.shape[2], block_values.shape[3]
    live = slots * 3 // 4
    rows = pointers.shape[0] - 1
    own_blocks = features.shape[0] // block
    group_blocks = own_blocks * n_row
    chunks = features.shape[1] // LANES
    shard = rows // n_col
    cols = block_cols[0, 0] - lax.axis_index("col") * group_blocks
    ids = jnp.arange(slots, dtype=jnp.int32)
    begins = jnp.any(pointers[:, None] == ids[None, :], axis=0)
    keep = jnp.where(begins, 0.0, 1.0).astype(jnp.float32)
    last = jnp.maximum(pointers[1:] - 1, 0)
    filled = (pointers[1:] > pointers[:-1]).astype(jnp.float32)
    smem = pl.BlockSpec(memory_space=pltpu.SMEM)
    hbm = pl.BlockSpec(memory_space=pl.ANY)
    messages = (2, chunks, n_col)
    result = pl.pallas_call(
        functools.partial(kernel, n_row, n_col),
        out_shape=jax.ShapeDtypeStruct((shard, block, features.shape[1]), jnp.bfloat16),
        in_specs=[smem] * 4 + [hbm] * 2,
        out_specs=pl.BlockSpec(memory_space=pltpu.VMEM),
        scratch_shapes=[
            [pltpu.VMEM((group_blocks, block, LANES), jnp.bfloat16)] * chunks,
            pltpu.VMEM((live, block, block), jnp.bfloat16),
            pltpu.VMEM((chunks, live, block, LANES), jnp.float32),
            pltpu.VMEM(messages + (shard, block, LANES), jnp.int16),
            pltpu.VMEM(messages + (shard, block, LANES), jnp.int16),
            pltpu.VMEM(messages + (shard, LANES), jnp.float32),
            pltpu.VMEM(messages + (shard, LANES), jnp.float32),
            pltpu.SemaphoreType.DMA((chunks + 1,)),
            pltpu.SemaphoreType.DMA((chunks, n_row // 2)),
            pltpu.SemaphoreType.DMA((chunks, n_row // 2)),
            pltpu.SemaphoreType.DMA((chunks, n_row // 2)),
            pltpu.SemaphoreType.DMA((chunks, n_row // 2)),
            pltpu.SemaphoreType.DMA(messages),
            pltpu.SemaphoreType.DMA(messages),
            pltpu.SemaphoreType.DMA(messages),
            pltpu.SemaphoreType.DMA(messages),
        ],
        compiler_params=pltpu.CompilerParams(
            collective_id=0, has_side_effects=True, vmem_limit_bytes=67043328
        ),
    )(cols, keep, last, filled, features.reshape(own_blocks, block, -1), block_values)
    return result.reshape(shard * block, -1)


def solution(mesh):
    return jax.shard_map(
        functools.partial(local, mesh.shape["row"], mesh.shape["col"]),
        mesh=mesh,
        in_specs=(
            P(("col", "row"), None),
            P("row", "col", None, None, None),
            P("row", "col", None),
            P("row", "col", None),
        ),
        out_specs=P(("row", "col"), None),
        check_vma=False,
    )
```

time: 295 us -> 124 us (0.42)
  waiting for transfers between devices: 203 us -> 0 us
  Pallas kernels: 0 us -> 117 us
  local copies, waits for them, and re-layouts: 45.4 us -> 2.26 us
  matrix products: 29.5 us -> 0 us
  between operations: 13.4 us -> 0.01 us
    reduce_scatter x1 -> x0, waiting for transfers between devices: 145 us -> none  [local(): lax.psum_scatter(partial_value, 'col', scatter_dimension=0, tiled=True)]
    pallas_call x0 -> x1, Pallas kernels: none -> 117 us  [local(): pl.pallas_call(functools.partial(kernel, n_row, n_col), out_shape=jax.Sha...]
    all_gather x1 -> x0, waiting for transfers between devices: 57.4 us -> none  [local(): panel = lax.all_gather(features, 'row', axis=0, tiled=True)]
    dot_general x2 -> x0, local copies, waits for them, and re-layouts: 33 us -> none  [the longest x1 24.9 us: local(): jnp.einsum('sij,sjk->sik', values, blocks, preferred_element_type=jnp.flo...]
    dot_general x2 -> x0, matrix products: 29.5 us -> none  [the longest x1 15.7 us: local(): jnp.einsum('rs,sik->rik', weights, products, precision=lax.Precision.HIGH...]
    gather x1 -> x0, local copies, waits for them, and re-layouts: 11.7 us -> none  [local(): blocks = panel_blocks[columns]]
  transfers between devices with their start and end apart: 2 -> 0, of which waited for: 2 -> 0; matrix products, arithmetic and copies ran while one was open for 1% -> 0% of each run, Pallas kernels for 0% -> 0%
where the time goes in v1:
time: 124 us
  Pallas kernels  117 us (94%)
  other arithmetic  5.16 us (4%)
  local copies, waits for them, and re-layouts  2.26 us (2%)
    pallas_call x1, Pallas kernels, local(): pl.pallas_call(functools.partial(kernel, n_row, n_col), out_shape=jax.Sha...  117 us

profile of v1, /device:TPU:0, one launch (start us, length us, event | category | flops | bytes accessed | tf_op | source)
XLA Modules:
  0.0 124.2 jit_solution(2115620381395542472)
XLA Ops:
  0.0 1.2 %broadcast_subtract_fusion = s32[1,1,192]{2,1,0:T(1,128)} fusion(s32[1,1,192]{2,1,0:T(1,128)} %param.7, s32[]{:T(128)S(6)} %mul.3), kind=kLoop, calls=%fused_computation.6 | loop fusion | flops 192 | bytes 1540 | tf_op jit(solution)/shard_map/sub | solution.py:231
  1.2 0.7 fusion
  2.0 0.6 broadcast_select_fusion.keep
  2.6 1.3 %fusion.1.filled = f32[64]{0:T(128)} fusion(s32[1,1,65]{2,1,0:T(1,128)} %param.6), kind=kLoop, calls=%fused_computation.3 | loop fusion | flops 128 | bytes 768 | tf_op jit(solution)/shard_map/convert_element_type | solution.py:236
  3.9 1.2 maximum_bitcast_fusion.last
  5.2 116.8 %shard_map.46 = bf16[16,128,256]{2,1,0:T(8,128)(2,1)} custom-call(s32[192]{0:T(256)} %bitcast.10, f32[192]{0:T(256)} %broadcast_select_fusion.keep, s32[64]{0:T(128)} %maximum_bitcast_fusion.last, f32[64]{0:T(128)} %fusion.1.filled, bf16[16,128,256]{2,1,0:T(8,128)(2,1)} %bitcast.9, bf16[1,1,192,128,128]{4,3,2,1,0:T(8,128)(2,1)} %values_hbm.1), custom_call_target="tpu_custom_call" | custom-call | tf_op jit(solution)/shard_map/pallas_call | solution.py:240
  122.0 2.3 %copy.6 = bf16[2048,256]{1,0:T(8,128)(2,1)} copy(bf16[2048,256]{1,0:T(8,128)(2,1)} %bitcast.8) | data formatting | bytes 2097152

commit v2 on v1

v2 whole, which is shorter than its diff:
```python
import functools

import jax
import jax.numpy as jnp
from jax import lax
from jax.experimental import pallas as pl
from jax.experimental.pallas import tpu as pltpu
from jax.sharding import PartitionSpec as P

LANES = 128
TOP = 32767.0
RIGHT, LEFT = 0, 1


def kernel(
    n_row, n_col, pointers, block_cols, features, values_hbm, out,
    panels, values, keep, sums, send_q, recv_q, send_s, recv_s,
    local_sem, ag_send, ag_recv, pair_send, pair_recv, rs_send, rs_recv, sc_send, sc_recv,
):
    n_chips = n_row // 2
    own_blocks = features.shape[0]
    half = own_blocks // 2
    chunks = len(panels)
    live = values.shape[0]
    shard = out.shape[0]
    parts, width = send_s.shape[3], send_s.shape[4]
    r, c = lax.axis_index("row"), lax.axis_index("col")
    chip, core = r // 2, r % 2
    square = n_chips == 4
    first_block = c * (own_blocks * n_row)

    def chip_to(o):
        if square:
            y, x = chip // 2, chip % 2
            return (1 - y if o >= 2 else y) * 2 + (1 - x if o % 2 else x)
        return (chip + o) % n_chips

    def chip_from(o):
        return chip_to(o) if square else (chip + n_chips - o) % n_chips

    partner = chip * 2 + 1 - core
    direct = (1, 2) if square else tuple(range(1, n_chips))

    def slot(k, row, h):
        return panels[k].at[pl.ds(row * own_blocks + h * half, half)]

    own = [
        pltpu.make_async_copy(
            features.at[:, :, pl.ds(k * LANES, LANES)],
            panels[k].at[pl.ds(r * own_blocks, own_blocks)],
            local_sem.at[k],
        )
        for k in range(chunks)
    ]
    for copy in own:
        copy.start()
    fetch = pltpu.make_async_copy(
        values_hbm.at[0, 0, pl.ds(0, live)], values, local_sem.at[chunks]
    )
    fetch.start()

    barrier = pltpu.get_barrier_semaphore()

    def greet(**where):
        pl.semaphore_signal(
            barrier, inc=1, device_id=where, device_id_type=pl.DeviceIdType.MESH
        )

    for o in direct:
        greet(row=chip_to(o) * 2 + core)
    greet(row=partner)
    pl.when(c > 0)(lambda: greet(col=c - 1))
    pl.when(c < n_col - 1)(lambda: greet(col=c + 1))
    ends = jnp.where(c > 0, 1, 0) + jnp.where(c < n_col - 1, 1, 0)
    pl.semaphore_wait(barrier, len(direct) + 1 + ends)

    def remote(src, dst, send, recv, **where):
        return pltpu.make_async_remote_copy(
            src_ref=src, dst_ref=dst, send_sem=send, recv_sem=recv,
            device_id=where, device_id_type=pl.DeviceIdType.MESH,
        )

    def piece(k, o, h, source, to):
        return remote(
            slot(k, source * 2 + core, h), slot(k, source * 2 + core, h),
            ag_send.at[k, o, h], ag_recv.at[k, o, h], row=to * 2 + core,
        )

    def across(k, o, h):
        return piece(k, o, h, chip, chip_to(o))

    def arriving(k, o, h):
        return piece(k, o, h, chip_from(o), chip_from(o))

    def relay(k, h):
        return piece(k, 3, h, chip_from(1 + h), chip_to(2 - h))

    def pair(k, o, h, whose):
        row = (chip_from(o) if o else chip) * 2 + whose
        return remote(
            slot(k, row, h), slot(k, row, h), pair_send.at[k, o, h], pair_recv.at[k, o, h],
            row=partner,
        )

    if square:
        order = ((1, 0), (2, 1), (1, 1), (2, 0))
    else:
        order = tuple((o, h) for o in direct for h in range(2))

    def gather_start(k):
        own[k].wait()
        for o, h in order:
            across(k, o, h).start()
        for h in range(2):
            pair(k, 0, h, core).start()

    def gather_finish(k):
        for o, h in order:
            arriving(k, o, h).wait_recv()
            if square and (o, h) in ((1, 0), (2, 1)):
                relay(k, h).start()
            pair(k, o, h, core).start()
        if square:
            for h in range(2):
                arriving(k, 3, h).wait_recv()
                pair(k, 3, h, core).start()
        for o in range(n_chips):
            for h in range(2):
                pair(k, o, h, 1 - core).wait_recv()

    unroll = 4 if live % 4 == 0 else 1

    def mark_rows():
        ids = lax.broadcasted_iota(jnp.int32, keep.shape, 0)

        def mark(q, flags):
            return jnp.where(ids == pointers[0, 0, q], 0.0, flags)

        keep[...] = lax.fori_loop(0, pointers.shape[2], mark, jnp.ones(keep.shape, jnp.float32))

    def compute(k):
        def step(i, total):
            first = i * unroll
            products = [
                jnp.dot(
                    values[first + u], panels[k][jnp.maximum(block_cols[0, 0, first + u] - first_block, 0)],
                    preferred_element_type=jnp.float32,
                )
                for u in range(unroll)
            ]
            for u in range(unroll):
                total = total * keep[pl.ds(first + u, 1), :] + products[u]
                sums[k, first + u] = total
            return total

        lax.fori_loop(0, live // unroll, step, jnp.zeros(sums.shape[2:], jnp.float32))

    def row_sum(k, q):
        begin, end = pointers[0, 0, q], pointers[0, 0, q + 1]
        return sums[k, jnp.maximum(end - 1, 0)] * jnp.where(end > begin, 1.0, 0.0)

    def received(way, k, j, s, b):
        levels = recv_q[way, k, j, s * width + b].astype(jnp.int32).astype(jnp.float32)
        return levels * recv_s[way, k, j, s, pl.ds(b, 1), :]

    def message(way, k, j, s):
        to = c + 1 if way == RIGHT else c - 1
        rows = pl.ds(s * width, width)
        return (
            remote(send_q.at[way, k, j, rows], recv_q.at[way, k, j, rows],
                   rs_send.at[way, k, j, s], rs_recv.at[way, k, j, s], col=to),
            remote(send_s.at[way, k, j, s], recv_s.at[way, k, j, s],
                   sc_send.at[way, k, j, s], sc_recv.at[way, k, j, s], col=to),
        )

    def forward(way, k, j, s, incoming):
        if incoming:
            for copy in message(way, k, j, s):
                copy.wait_recv()

        def one(b, carry):
            x = row_sum(k, j * shard + s * width + b)
            if incoming:
                x = x + received(way, k, j, s, b)
            most = jnp.maximum(jnp.max(jnp.abs(x), axis=0, keepdims=True), 1e-30)
            send_s[way, k, j, s, pl.ds(b, 1), :] = most * (1.0 / TOP)
            levels = jnp.round(x * (TOP / most)).astype(jnp.int32)
            send_q[way, k, j, s * width + b] = levels.astype(jnp.int16)
            return carry

        lax.fori_loop(0, width, one, 0)
        for copy in message(way, k, j, s):
            copy.start()

    def scatter_ends(k):
        def right(m, carry):
            forward(RIGHT, k, n_col - 1 - m // parts, m % parts, False)
            return carry

        def left(m, carry):
            forward(LEFT, k, m // parts, m % parts, False)
            return carry

        total = (n_col - 1) * parts

        @pl.when(c == 0)
        def _():
            lax.fori_loop(0, total, right, 0)

        @pl.when(c == n_col - 1)
        def _():
            lax.fori_loop(0, total, left, 0)

    def scatter_middle(k):
        def unit(n, carry):
            right = n - c
            left = n - (n_col - 1 - c)

            @pl.when((c > 0) & (right >= 0) & (right < (n_col - 1 - c) * parts))
            def _():
                forward(RIGHT, k, n_col - 1 - right // parts, right % parts, True)

            @pl.when((c < n_col - 1) & (left >= 0) & (left < c * parts))
            def _():
                forward(LEFT, k, left // parts, left % parts, True)

            return carry

        lax.fori_loop(1, (n_col - 2) * parts + 1, unit, 0)

    def finish(k):
        def write(ways):
            def part(s, carry):
                for way in ways:
                    for copy in message(way, k, c, s):
                        copy.wait_recv()

                def one(b, inner):
                    x = row_sum(k, c * shard + s * width + b)
                    for way in ways:
                        x = x + received(way, k, c, s, b)
                    out[s * width + b, :, pl.ds(k * LANES, LANES)] = x.astype(out.dtype)
                    return inner

                return lax.fori_loop(0, width, one, carry)

            lax.fori_loop(0, parts, part, 0)

        pl.when(c == 0)(lambda: write((LEFT,)))
        pl.when(c == n_col - 1)(lambda: write((RIGHT,)))
        pl.when((c > 0) & (c < n_col - 1))(lambda: write((RIGHT, LEFT)))

    gather_start(0)
    mark_rows()
    fetch.wait()
    gather_finish(0)
    for k in range(chunks):
        if k + 1 < chunks:
            gather_start(k + 1)
        compute(k)
        scatter_ends(k)
        if k > 0:
            scatter_middle(k - 1)
            finish(k - 1)
        if k + 1 < chunks:
            gather_finish(k + 1)
    scatter_middle(chunks - 1)
    finish(chunks - 1)

    for k in range(chunks):
        for h in range(2):
            for o in direct:
                across(k, o, h).wait_send()
            if square:
                relay(k, h).wait_send()
            for o in range(n_chips):
                pair(k, o, h, core).wait_send()
        for way in (RIGHT, LEFT):
            def drain(m, carry, way=way, k=k):
                j = m // parts

                @pl.when((j > c) if way == RIGHT else (j < c))
                def _():
                    for copy in message(way, k, j, m % parts):
                        copy.wait_send()

                return carry

            lax.fori_loop(0, n_col * parts, drain, 0)


def local(n_row, n_col, features, block_values, row_ptr, block_cols):
    slots, block = block_values.shape[2], block_values.shape[3]
    live = slots * 3 // 4
    own_blocks = features.shape[0] // block
    group_blocks = own_blocks * n_row
    chunks = features.shape[1] // LANES
    shard = (row_ptr.shape[2] - 1) // n_col
    parts = 4 if shard % 4 == 0 else 1
    smem = pl.BlockSpec(memory_space=pltpu.SMEM)
    hbm = pl.BlockSpec(memory_space=pl.ANY)
    messages = (2, chunks, n_col)
    gathers = (chunks, n_row // 2, 2)
    result = pl.pallas_call(
        functools.partial(kernel, n_row, n_col),
        out_shape=jax.ShapeDtypeStruct((shard, block, features.shape[1]), jnp.bfloat16),
        in_specs=[smem] * 2 + [hbm] * 2,
        out_specs=pl.BlockSpec(memory_space=pltpu.VMEM),
        scratch_shapes=[
            [pltpu.VMEM((group_blocks, block, LANES), jnp.bfloat16)] * chunks,
            pltpu.VMEM((live, block, block), jnp.bfloat16),
            pltpu.VMEM((live, LANES), jnp.float32),
            pltpu.VMEM((chunks, live, block, LANES), jnp.float32),
            pltpu.VMEM(messages + (shard, block, LANES), jnp.int16),
            pltpu.VMEM(messages + (shard, block, LANES), jnp.int16),
            pltpu.VMEM(messages + (parts, shard // parts, LANES), jnp.float32),
            pltpu.VMEM(messages + (parts, shard // parts, LANES), jnp.float32),
            pltpu.SemaphoreType.DMA((chunks + 1,)),
        ]
        + [pltpu.SemaphoreType.DMA(gathers)] * 4
        + [pltpu.SemaphoreType.DMA(messages + (parts,))] * 4,
        compiler_params=pltpu.CompilerParams(
            collective_id=0, has_side_effects=True, vmem_limit_bytes=67043328
        ),
    )(row_ptr, block_cols, features.reshape(own_blocks, block, -1), block_values)
    return result.reshape(shard * block, -1)


def solution(mesh):
    return jax.shard_map(
        functools.partial(local, mesh.shape["row"], mesh.shape["col"]),
        mesh=mesh,
        in_specs=(
            P(("col", "row"), None),
            P("row", "col", None, None, None),
            P("row", "col", None),
            P("row", "col", None),
        ),
        out_specs=P(("row", "col"), None),
        check_vma=False,
    )
```

time: 124 us -> 109 us (0.88); the launches traced: 124 us -> 107 us
  Pallas kernels: 117 us -> 105 us
  other arithmetic: 5.16 us -> 0 us
    pallas_call x1, Pallas kernels: 117 us -> 105 us  [local(): pl.pallas_call(functools.partial(kernel, n_row, n_col), out_shape=jax.Sha...]
    convert_element_type x1 -> x0, other arithmetic: 1.34 us -> none  [local(): filled = (pointers[1:] > pointers[:-1]).astype(jnp.float32)]
    sub x1 -> x0, other arithmetic: 1.24 us -> none  [local(): cols = block_cols[0, 0] - lax.axis_index('col') * group_blocks]
where the time goes in v2:
time: 109 us; the launch traced here: 107 us
  Pallas kernels  105 us (96%)
  local copies, waits for them, and re-layouts  2.26 us (2%)
    pallas_call x1, Pallas kernels, local(): pl.pallas_call(functools.partial(kernel, n_row, n_col), out_shape=jax.Sha...  105 us
    unnamed x1, local copies, waits for them, and re-layouts  2.26 us

profile of v2, /device:TPU:0, one launch (start us, length us, event | category | flops | bytes accessed | tf_op | source)
XLA Modules:
  0.0 107.3 jit_solution(317353132084701581)
XLA Ops:
  0.0 105.0 %shard_map.46 = bf16[16,128,256]{2,1,0:T(8,128)(2,1)} custom-call(s32[1,1,65]{2,1,0:T(1,128)} %pointers.1, s32[1,1,192]{2,1,0:T(1,128)} %block_cols.1, bf16[16,128,256]{2,1,0:T(8,128)(2,1)} %bitcast.3, bf16[1,1,192,128,128]{4,3,2,1,0:T(8,128)(2,1)} %values_hbm.1), custom_call_target="tpu_custom_call" | custom-call | tf_op jit(solution)/shard_map/pallas_call | solution.py:304
  105.1 2.3 %copy.6 = bf16[2048,256]{1,0:T(8,128)(2,1)} copy(bf16[2048,256]{1,0:T(8,128)(2,1)} %bitcast.2) | data formatting | bytes 2097152
